TPU v7x, 32 devices: a whole 2x2x4 slice. The times are simulated.
32 devices in a mesh: gx: 4 (over z), gy: 8 (over y, x, core).
Axes of the slice: x: 2, y: 2, z: 4, core: 2. Of those that a mesh axis runs over, the one named last changes fastest.
Arguments:
- tables: float32 [2, 262144, 128], P(None, ('gx', 'gy')), may hold values from -0.9 to 0.9
- cold_rows: int32 [32, 2, 32, 16], P(('gx', 'gy')), may hold values from 0 to 8191, as said below
- cold_bags: int32 [32, 2, 32, 16], P(('gx', 'gy')), may hold values from -1 to 127, as said below
- hot_rows: int32 [2, 256], replicated, may hold values from 0 to 262143
- hot_ids: int32 [4096, 2, 8], P(('gx', 'gy')), may hold values from 0 to 255
Outputs:
- pooled: float32 [4096, 2, 128], P(('gx', 'gy'))
Inputs may be any that keep to these rules, and one draw needn't show every extreme that they name: `cold_rows`: every entry names one of the owner's 8192 rows. `cold_bags`: live slots of one sender, table and owner come first, the empty ones (-1) after them; in every draw each table has an owner whose 16 slots are all live from every sender.
All inputs are finite; a program needn't handle non-finite values.
Results may differ from a plain program's by a relative error of at most 0.0003.
Values sent between devices are 32-bit elements; how exact they have to be, the bound alone decides.
No kernel may reach another device: no remote copies, remote signals or barrier semaphores. Data moves between devices by JAX's collectives and lax.ppermute only.
A program may use at most 64 MiB of HBM per device.

v0:
```python
import math
import jax
import jax.numpy as jnp
from jax import lax
from jax.sharding import PartitionSpec as P


def pick_rows(table, indices):
    count = indices.shape[0]
    block = math.gcd(512, count)
    row_ids = jnp.arange(table.shape[0], dtype=jnp.int32)
    grouped = indices.reshape(count // block, block)

    def one_block(wanted):
        selector = (wanted[:, None] == row_ids[None, :]).astype(jnp.float32)
        return jnp.dot(
            selector, table, precision=lax.Precision.HIGHEST, preferred_element_type=jnp.float32
        )

    return lax.map(one_block, grouped).reshape(count, table.shape[1])


def body(tables, cold_rows, cold_bags, hot_rows, hot_ids):
    axis_x = lax.axis_size("gx")
    axis_y = lax.axis_size("gy")
    peer_count = axis_x * axis_y
    table_count, rows_dev, emb_width = tables.shape
    slot_cap = cold_rows.shape[3]
    batch_rows = hot_ids.shape[0]
    hot_count = hot_rows.shape[1]
    my_index = lax.axis_index(("gx", "gy"))
    hot_owner = hot_rows // rows_dev
    local_rows = jnp.where(hot_owner == my_index, hot_rows - my_index * rows_dev, -1)
    picked = jax.vmap(pick_rows)(tables, local_rows)
    hot_table = lax.psum(picked, ("gx", "gy"))
    matches = jnp.sum(
        (
            hot_ids[:, :, :, None] == jnp.arange(hot_count, dtype=jnp.int32)[None, None, None, :]
        ).astype(jnp.float32),
        axis=2,
    )
    hot_part = jnp.einsum("bth,thd->btd", matches, hot_table, precision=lax.Precision.HIGHEST)
    my_rows = cold_rows[0]
    my_bags = cold_bags[0]
    got_rows, got_bags = (
        lax.all_to_all(my_rows, ("gx", "gy"), split_axis=1, concat_axis=1, tiled=True),
        lax.all_to_all(my_bags, ("gx", "gy"), split_axis=1, concat_axis=1, tiled=True),
    )
    wanted_rows = jnp.where(got_bags >= 0, got_rows, -1)
    looked = jax.vmap(pick_rows)(tables, wanted_rows.reshape(table_count, -1))
    looked = looked.reshape(table_count, peer_count, slot_cap, emb_width)
    samples = jnp.arange(batch_rows, dtype=jnp.int32)
    returned = lax.all_to_all(looked, ("gx", "gy"), split_axis=1, concat_axis=1, tiled=True)
    onehot = (my_bags[:, None, :, :] == samples[None, :, None, None]).astype(jnp.float32)
    cold_part = jnp.einsum("tbpc,tpcd->btd", onehot, returned, precision=lax.Precision.HIGHEST)
    return cold_part + hot_part


def solution(mesh):
    return jax.shard_map(
        body,
        mesh=mesh,
        in_specs=(
            P(None, ("gx", "gy"), None),
            P(("gx", "gy"), None, None, None),
            P(("gx", "gy"), None, None, None),
            P(),
            P(("gx", "gy"), None, None),
        ),
        out_specs=P(("gx", "gy"), None, None),
        check_vma=False,
    )
```

profile of v0, /device:TPU:0, one launch (start us, length us, event | category | flops | bytes accessed | tf_op | source)
XLA Modules:
  0.0 203.2 jit_solution(9199264976657592994)
XLA Ops:
  6.5 1.4 copy.23
  7.9 7.3 %all-to-all-start.1 = ((s32[2,32,16]{2,0,1:T(2,128)}), s32[2,32,16]{2,0,1:T(2,128)S(1)}, u32[]{:S(2)}, u32[]{:S(2)}) async-start(s32[2,32,16]{2,0,1:T(2,128)} %bitcast.1), calls=%async_computation.1 | async-start | bytes 65536 | tf_op jit(solution)/shard_map/all_to_all | solution.py:46
  15.3 1.4 copy.22
  16.7 5.9 %all-to-all-done.1 = s32[2,32,16]{2,0,1:T(2,128)S(1)} async-done(((s32[2,32,16]{2,0,1:T(2,128)}), s32[2,32,16]{2,0,1:T(2,128)S(1)}, u32[]{:S(2)}, u32[]{:S(2)}) %all-to-all-start.1) | async-done | bytes 4128 | tf_op jit(solution)/shard_map/all_to_all | solution.py:46
  22.5 2.6 %all-to-all-start = ((s32[2,32,16]{2,0,1:T(2,128)}), s32[2,32,16]{2,0,1:T(2,128)S(1)}, u32[]{:S(2)}, u32[]{:S(2)}) async-start(s32[2,32,16]{2,0,1:T(2,128)} %bitcast), calls=%async_computation | async-start | bytes 65536 | tf_op jit(solution)/shard_map/all_to_all | solution.py:47
  25.1 7.2 %all-to-all-done = s32[2,32,16]{2,0,1:T(2,128)S(1)} async-done(((s32[2,32,16]{2,0,1:T(2,128)}), s32[2,32,16]{2,0,1:T(2,128)S(1)}, u32[]{:S(2)}, u32[]{:S(2)}) %all-to-all-start) | async-done | bytes 4128 | tf_op jit(solution)/shard_map/all_to_all | solution.py:47
  32.4 0.1 eq.74
  32.5 0.0 copy-start.1
  32.5 18.0 %fusion = f32[2,512,128]{2,1,0:T(8,128)S(1)} fusion(f32[2,8192,128]{2,1,0:T(8,128)} %param.5, s32[2,512]{1,0:T(2,128)S(1)} %eq.74), kind=kOutput, calls=%fused_computation.1 | convolution fusion | flops 12893290496 | bytes 8916992 | tf_op jit(solution)/shard_map/vmap()/while/body/eval_jaxpr/dot_general | solution.py:16
  50.5 0.0 copy-start
  50.5 0.9 copy.25
  51.4 2.6 %all-to-all-start.2 = ((f32[2,32,16,128]{3,2,0,1:T(8,128)}), f32[2,32,16,128]{3,2,0,1:T(8,128)S(1)}, u32[]{:S(2)}, u32[]{:S(2)}) async-start(f32[2,32,16,128]{3,2,0,1:T(8,128)} %copy.25), calls=%async_computation.2 | async-start | bytes 1048576 | tf_op jit(solution)/shard_map/all_to_all | solution.py:53
  54.0 0.2 all-reduce.2.cloned.1.call-start
  54.2 0.0 copy-done.1
  54.3 11.7 %fusion.2 = f32[2,256,128]{2,1,0:T(8,128)} fusion(f32[2,8192,128]{2,1,0:T(8,128)} %param.5, s32[2,256]{1,0:T(2,128)S(1)} %compare_select_fusion.1), kind=kOutput, calls=%fused_computation.4 | convolution fusion | flops 6446645248 | bytes 8652800 | tf_op jit(solution)/shard_map/vmap()/while/body/eval_jaxpr/dot_general | solution.py:16
  66.0 0.0 all-reduce.2.cloned.1.call-update
  66.0 0.0 copy-done
  66.0 0.1 copy.26
  66.2 0.8 convert_reduce_fusion
  67.0 2.6 %all-to-all-done.2 = f32[2,32,16,128]{3,2,0,1:T(8,128)S(1)} async-done(((f32[2,32,16,128]{3,2,0,1:T(8,128)}), f32[2,32,16,128]{3,2,0,1:T(8,128)S(1)}, u32[]{:S(2)}, u32[]{:S(2)}) %all-to-all-start.2) | async-done | bytes 524320 | tf_op jit(solution)/shard_map/all_to_all | solution.py:53
  69.6 1.5 convolution_bitcast_fusion
  71.1 122.8 %all-reduce.2.cloned.1.call-done = f32[2,256,128]{2,1,0:T(8,128)} async-done(((f32[2,256,128]{2,1,0:T(8,128)}), f32[2,256,128]{2,1,0:T(8,128)}) %all-reduce.2.cloned.1.call-update) | async-done | bytes 262160 | tf_op jit(solution)/shard_map/psum | solution.py:35
  194.0 1.6 fusion.4
  195.6 0.8 copy.29
  (3 shorter events, 0.0 us)
Async XLA Ops:
  7.9 14.6 %all-to-all-start.1 = ((s32[2,32,16]{2,0,1:T(2,128)}), s32[2,32,16]{2,0,1:T(2,128)S(1)}, u32[]{:S(2)}, u32[]{:S(2)}) async-start(s32[2,32,16]{2,0,1:T(2,128)} %bitcast.1), calls=%async_computation.1 | async-start | bytes 65536 | tf_op jit(solution)/shard_map/all_to_all | solution.py:46
  22.5 9.8 %all-to-all-start = ((s32[2,32,16]{2,0,1:T(2,128)}), s32[2,32,16]{2,0,1:T(2,128)S(1)}, u32[]{:S(2)}, u32[]{:S(2)}) async-start(s32[2,32,16]{2,0,1:T(2,128)} %bitcast), calls=%async_computation | async-start | bytes 65536 | tf_op jit(solution)/shard_map/all_to_all | solution.py:47
  32.5 21.8 %copy-start.1 = (s32[2,256]{1,0:T(2,128)S(1)}, s32[2,256]{1,0:T(2,128)}, u32[]{:S(2)}) copy-start(s32[2,256]{1,0:T(2,128)} %param.8) | copy-start | bytes 6148
  50.5 15.5 %copy-start = (s32[128,2,8]{0,2,1:T(8,128)S(1)}, s32[128,2,8]{0,2,1:T(8,128)}, u32[]{:S(2)}) copy-start(s32[128,2,8]{0,2,1:T(8,128)} %param.9) | copy-start | bytes 24580
  51.4 18.2 %all-to-all-start.2 = ((f32[2,32,16,128]{3,2,0,1:T(8,128)}), f32[2,32,16,128]{3,2,0,1:T(8,128)S(1)}, u32[]{:S(2)}, u32[]{:S(2)}) async-start(f32[2,32,16,128]{3,2,0,1:T(8,128)} %copy.25), calls=%async_computation.2 | async-start | bytes 1048576 | tf_op jit(solution)/shard_map/all_to_all | solution.py:53
  54.0 140.0 %all-reduce.2.cloned.1.call-start = ((), (), s32[]{:S(2)}) async-start(), calls=%async_computation.3 | async-start | bytes 524288 | tf_op jit(solution)/shard_map/psum | solution.py:35
Sparse Core Ops, SparseCore 0:
  66.1 127.7 all-reduce.1
where the time goes:
time: 204 us; the launch traced here: 203 us
  waiting for transfers between devices  139 us (68%)
  matrix products  32.8 us (16%)
  between operations  13.5 us (7%)
  starting transfers between devices  12.7 us (6%)
  local copies, waits for them, and re-layouts  4.66 us (2%)
    psum x1, waiting for transfers between devices, body(): hot_table = lax.psum(picked, ('gx', 'gy'))  123 us
    dot_general x2, matrix products, one_block(): jnp.dot(selector, table, precision=lax.Precision.HIGHEST, preferred_eleme...  29.7 us
    all_to_all x1, starting transfers between devices, body(): lax.all_to_all(my_rows, ('gx', 'gy'), split_axis=1, concat_axis=1, tiled=...  7.33 us
    all_to_all x1, waiting for transfers between devices, body(): lax.all_to_all(my_bags, ('gx', 'gy'), split_axis=1, concat_axis=1, tiled=...  7.25 us
    all_to_all x1, waiting for transfers between devices, body(): lax.all_to_all(my_rows, ('gx', 'gy'), split_axis=1, concat_axis=1, tiled=...  5.86 us
  transfers between devices with their start and end apart: 4, of which 4 were waited for; matrix products, arithmetic and copies ran while one was open for 8% of the time, Pallas kernels for 0%

commit v1 on v0

--- a/solution.py
+++ b/solution.py
@@ -43,7 +43,15 @@
     my_rows = cold_rows[0]
     my_bags = cold_bags[0]
     got_rows, got_bags = (
-        lax.all_to_all(my_rows, ("gx", "gy"), split_axis=1, concat_axis=1, tiled=True),
+        jnp.concatenate(
+            lax.all_to_all(
+                jnp.stack(jnp.split(my_rows, lax.axis_size(("gx", "gy")), axis=1)),
+                ("gx", "gy"),
+                0,
+                0,
+            ),
+            axis=1,
+        ),
         lax.all_to_all(my_bags, ("gx", "gy"), split_axis=1, concat_axis=1, tiled=True),
     )
     wanted_rows = jnp.where(got_bags >= 0, got_rows, -1)

time: 204 us -> 225 us (1.10)
  local copies, waits for them, and re-layouts: 4.66 us -> 25.7 us
    unnamed x7 -> x37, local copies, waits for them, and re-layouts: 2.96 us -> 19.3 us
    split x0 -> x2, local copies, waits for them, and re-layouts: none -> 4.08 us  [body(): jnp.split(my_rows, lax.axis_size(('gx', 'gy')), axis=1)]
  transfers between devices with their start and end apart: 4 -> 4, of which waited for: 4 -> 4; matrix products, arithmetic and copies ran while one was open for 8% -> 7% of each run, Pallas kernels for 0% -> 0%
where the time goes in v1:
time: 225 us; the launch traced here: 224 us
  waiting for transfers between devices  139 us (62%)
  matrix products  32.8 us (15%)
  local copies, waits for them, and re-layouts  25.7 us (11%)
  between operations  13.5 us (6%)
  starting transfers between devices  12.7 us (6%)
    psum x1, waiting for transfers between devices, body(): hot_table = lax.psum(picked, ('gx', 'gy'))  123 us
    dot_general x2, matrix products, one_block(): jnp.dot(selector, table, precision=lax.Precision.HIGHEST, preferred_eleme...  29.8 us
    unnamed x37, local copies, waits for them, and re-layouts  19.3 us
    all_to_all x1, starting transfers between devices, body(): lax.all_to_all(jnp.stack(jnp.split(my_rows, lax.axis_size(('gx', 'gy')),...  7.33 us
    all_to_all x1, waiting for transfers between devices, body(): lax.all_to_all(my_bags, ('gx', 'gy'), split_axis=1, concat_axis=1, tiled=...  7.25 us
    all_to_all x1, waiting for transfers between devices, body(): lax.all_to_all(jnp.stack(jnp.split(my_rows, lax.axis_size(('gx', 'gy')),...  5.85 us
  transfers between devices with their start and end apart: 4, of which 4 were waited for; matrix products, arithmetic and copies ran while one was open for 7% of the time, Pallas kernels for 0%

profile of v1, /device:TPU:0, one launch (start us, length us, event | category | flops | bytes accessed | tf_op | source)
XLA Modules:
  0.0 224.3 jit_solution(7283428008566855628)
XLA Ops:
  6.5 1.8 slice_reduce_fusion.19
  8.4 2.3 %slice_reduce_fusion = (s32[2,16]{1,0:T(2,128)S(1)}, s32[2,16]{1,0:T(2,128)S(1)}, s32[2,16]{1,0:T(2,128)S(1)}, s32[2,16]{1,0:T(2,128)S(1)}, s32[2,16]{1,0:T(2,12...) fusion(s32[2,32,16]{1,2,0:T(8,128)} %bitcast.80), kind=kLoop, calls=%fused_computation.47 | loop fusion | bytes 4864 | tf_op jit(solution)/shard_map/split | solution.py:48
  10.6 0.6 constant_dynamic-update-slice_fusion.31
  11.2 0.6 constant_dynamic-update-slice_fusion.30
  11.8 0.6 constant_dynamic-update-slice_fusion.29
  13.0 0.6 constant_dynamic-update-slice_fusion.27
  14.7 0.6 constant_dynamic-update-slice_fusion.24
  17.0 0.6 constant_dynamic-update-slice_fusion.20
  18.7 0.6 constant_dynamic-update-slice_fusion.17
  20.4 0.6 constant_dynamic-update-slice_fusion.14
  22.1 0.6 constant_dynamic-update-slice_fusion.11
  22.7 0.6 constant_dynamic-update-slice_fusion.10
  24.4 0.6 constant_dynamic-update-slice_fusion.7
  25.5 0.6 constant_dynamic-update-slice_fusion.5
  26.1 0.6 constant_dynamic-update-slice_fusion.4
  27.8 0.6 constant_dynamic-update-slice_fusion.1
  28.4 0.6 constant_dynamic-update-slice_fusion
  29.0 7.3 %all-to-all-start.1 = ((s32[32,2,1,16]{3,1,2,0:T(2,128)}), s32[32,2,1,16]{3,1,2,0:T(2,128)S(1)}, u32[]{:S(2)}, u32[]{:S(2)}) async-start(s32[32,2,1,16]{3,1,2,0:T(2,128)} %constant_dynamic-update-slice_fusion), calls=%async_computation.1 | async-start | bytes 65536 | tf_op jit(solution)/shard_map/all_to_all | solution.py:47
  36.3 1.4 copy.25
  37.7 5.8 %all-to-all-done.1 = s32[32,2,1,16]{3,1,2,0:T(2,128)S(1)} async-done(((s32[32,2,1,16]{3,1,2,0:T(2,128)}), s32[32,2,1,16]{3,1,2,0:T(2,128)S(1)}, u32[]{:S(2)}, u32[]{:S(2)}) %all-to-all-start.1) | async-done | bytes 4128 | tf_op jit(solution)/shard_map/all_to_all | solution.py:47
  43.6 2.6 %all-to-all-start = ((s32[2,32,16]{2,0,1:T(2,128)}), s32[2,32,16]{2,0,1:T(2,128)S(1)}, u32[]{:S(2)}, u32[]{:S(2)}) async-start(s32[2,32,16]{2,0,1:T(2,128)} %bitcast), calls=%async_computation | async-start | bytes 65536 | tf_op jit(solution)/shard_map/all_to_all | solution.py:55
  46.2 7.2 %all-to-all-done = s32[2,32,16]{2,0,1:T(2,128)S(1)} async-done(((s32[2,32,16]{2,0,1:T(2,128)}), s32[2,32,16]{2,0,1:T(2,128)S(1)}, u32[]{:S(2)}, u32[]{:S(2)}) %all-to-all-start) | async-done | bytes 4128 | tf_op jit(solution)/shard_map/all_to_all | solution.py:55
  53.6 18.0 %fusion = f32[2,512,128]{2,1,0:T(8,128)S(1)} fusion(f32[2,8192,128]{2,1,0:T(8,128)} %param.5, s32[2,512]{1,0:T(2,128)S(1)} %eq.74), kind=kOutput, calls=%fused_computation.1 | convolution fusion | flops 12893290496 | bytes 8916992 | tf_op jit(solution)/shard_map/vmap()/while/body/eval_jaxpr/dot_general | solution.py:16
  71.6 0.9 copy.27
  72.5 2.6 %all-to-all-start.2 = ((f32[2,32,16,128]{3,2,0,1:T(8,128)}), f32[2,32,16,128]{3,2,0,1:T(8,128)S(1)}, u32[]{:S(2)}, u32[]{:S(2)}) async-start(f32[2,32,16,128]{3,2,0,1:T(8,128)} %copy.27), calls=%async_computation.2 | async-start | bytes 1048576 | tf_op jit(solution)/shard_map/all_to_all | solution.py:61
  75.4 11.7 %fusion.2 = f32[2,256,128]{2,1,0:T(8,128)} fusion(f32[2,8192,128]{2,1,0:T(8,128)} %param.5, s32[2,256]{1,0:T(2,128)S(1)} %compare_select_fusion.1), kind=kOutput, calls=%fused_computation.4 | convolution fusion | flops 6446645248 | bytes 8652800 | tf_op jit(solution)/shard_map/vmap()/while/body/eval_jaxpr/dot_general | solution.py:16
  87.3 0.8 convert_reduce_fusion
  88.1 2.6 %all-to-all-done.2 = f32[2,32,16,128]{3,2,0,1:T(8,128)S(1)} async-done(((f32[2,32,16,128]{3,2,0,1:T(8,128)}), f32[2,32,16,128]{3,2,0,1:T(8,128)S(1)}, u32[]{:S(2)}, u32[]{:S(2)}) %all-to-all-start.2) | async-done | bytes 524320 | tf_op jit(solution)/shard_map/all_to_all | solution.py:61
  90.7 1.5 convolution_bitcast_fusion
  92.2 122.9 %all-reduce.2.cloned.1.call-done = f32[2,256,128]{2,1,0:T(8,128)} async-done(((f32[2,256,128]{2,1,0:T(8,128)}), f32[2,256,128]{2,1,0:T(8,128)}) %all-reduce.2.cloned.1.call-update) | async-done | bytes 262160 | tf_op jit(solution)/shard_map/psum | solution.py:35
  215.1 1.6 fusion.4
  216.7 0.8 copy.31
  (28 shorter events, 10.1 us)
Async XLA Ops:
  29.0 14.6 %all-to-all-start.1 = ((s32[32,2,1,16]{3,1,2,0:T(2,128)}), s32[32,2,1,16]{3,1,2,0:T(2,128)S(1)}, u32[]{:S(2)}, u32[]{:S(2)}) async-start(s32[32,2,1,16]{3,1,2,0:T(2,128)} %constant_dynamic-update-slice_fusion), calls=%async_computation.1 | async-start | bytes 65536 | tf_op jit(solution)/shard_map/all_to_all | solution.py:47
  43.6 9.8 %all-to-all-start = ((s32[2,32,16]{2,0,1:T(2,128)}), s32[2,32,16]{2,0,1:T(2,128)S(1)}, u32[]{:S(2)}, u32[]{:S(2)}) async-start(s32[2,32,16]{2,0,1:T(2,128)} %bitcast), calls=%async_computation | async-start | bytes 65536 | tf_op jit(solution)/shard_map/all_to_all | solution.py:55
  53.5 21.8 %copy-start.1 = (s32[2,256]{1,0:T(2,128)S(1)}, s32[2,256]{1,0:T(2,128)}, u32[]{:S(2)}) copy-start(s32[2,256]{1,0:T(2,128)} %param.8) | copy-start | bytes 6148
  71.6 15.5 %copy-start = (s32[128,2,8]{0,2,1:T(8,128)S(1)}, s32[128,2,8]{0,2,1:T(8,128)}, u32[]{:S(2)}) copy-start(s32[128,2,8]{0,2,1:T(8,128)} %param.9) | copy-start | bytes 24580
  72.5 18.2 %all-to-all-start.2 = ((f32[2,32,16,128]{3,2,0,1:T(8,128)}), f32[2,32,16,128]{3,2,0,1:T(8,128)S(1)}, u32[]{:S(2)}, u32[]{:S(2)}) async-start(f32[2,32,16,128]{3,2,0,1:T(8,128)} %copy.27), calls=%async_computation.2 | async-start | bytes 1048576 | tf_op jit(solution)/shard_map/all_to_all | solution.py:61
  75.1 140.0 %all-reduce.2.cloned.1.call-start = ((), (), s32[]{:S(2)}) async-start(), calls=%async_computation.3 | async-start | bytes 524288 | tf_op jit(solution)/shard_map/psum | solution.py:35
Sparse Core Ops, SparseCore 0:
  87.2 127.8 all-reduce.1
